TPU v7x, 512 devices: a whole 4x4x16 slice. The times are simulated.
512 devices in a mesh: dp: 64 (over z_lo, x, core), ens: 8 (over y, z_hi).
Axes of the slice: x: 4, y: 4, z: 16 (z_hi: 2, z_lo: 8; z = z_hi * 8 + z_lo), core: 2. Of those that a mesh axis runs over, the one named last changes fastest.
Arguments:
- embeddings: bfloat16 [49152, 1024], P('dp'), may hold values from -6 to 6
- valid_mask: int32 [49152], P('dp'), may hold values 0 or 1
- first_weight: bfloat16 [8, 1024, 4096], P(None, 'dp', 'ens'), may hold values from -0.1875 to 0.1875
- second_weight: bfloat16 [8, 4096, 128], P(None, 'ens'), may hold values from -0.09375 to 0.09375
- thresholds: int32 [8], replicated, may hold values from -256 to 256
Outputs:
- mean_logits: float32 [49152, 128], P('dp')
- kept_share: float32 [8], P('ens')
- agree_share: float32 [8], P('ens')
All inputs are finite; a program needn't handle non-finite values. No bound on the sum of `valid_mask` on one device may be relied on, other than what follows from the above.
Results may differ from a plain program's by a relative error of at most 0.0044.
Values may be sent and summed in bfloat16 or wider, within the bound.
A program may use at most 64 MiB of HBM per device.

v0:
```python
import jax
import jax.numpy as jnp
from jax import lax
from jax.sharding import PartitionSpec as P


def split_up(shard, dim, size):
    shape = shard.shape
    blocks = shard.reshape(*shape[:dim], size, shape[dim] // size, *shape[dim + 1 :])
    return jnp.moveaxis(blocks, dim, 0)


def cut_rows(length, count):
    lap = length // count
    if lap >= 8:
        lap -= lap % 8
    return [lap * k for k in range(1, count)]


def in_order(blocks, dim):
    shape = list(blocks.shape[1:])
    shape[dim] *= blocks.shape[0]
    return jnp.moveaxis(blocks, 0, dim).reshape(shape)


def several_exchanges(shard, axis, pieces, split_dim, concat_dim):
    blocks = split_up(shard, split_dim, lax.axis_size(axis))
    split_at = max(range(1, max(2, blocks.ndim - 1)), key=lambda d: blocks.shape[d])
    done = []
    for section in jnp.split(blocks, cut_rows(blocks.shape[split_at], pieces), axis=split_at):
        if section.size:
            done.append(lax.all_to_all(section, axis, split_axis=0, concat_axis=0, tiled=True))
    return in_order(jnp.concatenate(done, axis=split_at), concat_dim)


def from_everyone(shard, axis):
    copies = jnp.broadcast_to(shard, (lax.axis_size(axis), *shard.shape))
    return lax.all_to_all(copies, axis, split_axis=0, concat_axis=0, tiled=True)


def over_copies(shard, axis):
    everything = from_everyone(shard, axis)
    return jnp.sum(everything.astype(jnp.float32), axis=0)


def of_everyone(shard, axis):
    return from_everyone(shard, axis).sum(axis=0)


def in_one(arrays, axis):
    ends = [0]
    for a in arrays:
        ends.append(ends[-1] + a.size)
    total = of_everyone(jnp.concatenate([a.ravel() for a in arrays]), axis)
    return tuple((total[b:e].reshape(a.shape) for a, b, e in zip(arrays, ends, ends[1:])))


def on_device(embeddings, valid_mask, first_weight, second_weight, thresholds):
    member = lax.axis_index("ens")
    own_first = lax.all_to_all(first_weight, "ens", split_axis=0, concat_axis=2, tiled=True)
    own_second = several_exchanges(second_weight, "ens", 2, 0, 1)
    full_first = lax.all_gather(own_first[0], "dp", axis=0, tiled=True)
    hidden = jnp.maximum(
        jnp.dot(embeddings, full_first, preferred_element_type=jnp.float32), 0.0
    ).astype(jnp.bfloat16)
    logits_own = jnp.dot(hidden, own_second[0], preferred_element_type=jnp.float32)
    classes = logits_own.shape[1]
    levels = jnp.arange(classes, dtype=jnp.float32)
    grades = (2.0 * levels / (classes - 1) - 1.0) * jnp.sqrt(jnp.float32(3.0 / classes))
    scores = jnp.dot(logits_own, grades, precision=lax.Precision.HIGHEST)
    cutoffs = thresholds.astype(jnp.float32) / 256.0
    own_cutoff = lax.dynamic_index_in_dim(cutoffs, member, 0, keepdims=False)
    validity = valid_mask.astype(jnp.float32)
    kept_soft = validity * jax.nn.sigmoid(4.0 * (scores - own_cutoff))
    mean_logits = (
        over_copies(logits_own.astype(jnp.bfloat16), "ens").astype(jnp.float32)
        / first_weight.shape[0]
    )
    ens_score = jnp.dot(mean_logits, grades, precision=lax.Precision.HIGHEST)
    ens_kept = jax.nn.sigmoid(4.0 * (ens_score - jnp.mean(cutoffs)))
    agree_local = jnp.sum(kept_soft * ens_kept)
    kept_total, agree_total = in_one((jnp.sum(kept_soft), agree_local), "dp")
    shard_docs = embeddings.shape[0]
    return (
        mean_logits,
        (kept_total / shard_docs).reshape(1),
        (agree_total / shard_docs).reshape(1),
    )


def solution(mesh):
    return jax.shard_map(
        on_device,
        mesh=mesh,
        in_specs=(P("dp", None), P("dp"), P(None, "dp", "ens"), P(None, "ens", None), P()),
        out_specs=(P("dp", None), P("ens"), P("ens")),
        check_vma=False,
    )
```

profile of v0, /device:TPU:1, one launch (start us, length us, event | category | flops | bytes accessed | tf_op | source)
XLA Modules:
  0.0 333.6 jit_solution(111445874965293776)
XLA Ops:
  7.2 0.0 copy-start
  7.2 0.0 all-gather.2.cloned.1.call-start
  7.2 32.7 %all_to_all.36 = bf16[8,16,512]{2,1,0:T(8,128)(2,1)S(1)} all-to-all(bf16[8,16,512]{2,1,0:T(8,128)(2,1)} %param.7), channel_id=1, replica_groups=mesh['dp'=64,'ens'=8] {'ens'}, dimensions={0} | all-to-all | bytes 262144 | tf_op jit(solution)/shard_map/all_to_all | solution.py:60
  39.9 0.7 copy.16
  40.5 0.0 all-gather.2.cloned.1.call-update
  40.6 1.3 fusion.12
  41.9 19.8 %all_to_all.37 = bf16[8,1,256,128]{3,2,1,0:T(8,128)(2,1)S(1)} all-to-all(bf16[8,1,256,128]{3,2,1,0:T(8,128)(2,1)S(1)} %get-tuple-element.6), channel_id=1, replica_groups=mesh['dp'=64,'ens'=8] {'ens'}, dimensions={0} | all-to-all | bytes 1048576 | tf_op jit(solution)/shard_map/all_to_all | solution.py:32
  61.7 27.5 %all_to_all.38 = bf16[8,1,256,128]{3,2,1,0:T(8,128)(2,1)S(1)} all-to-all(bf16[8,1,256,128]{3,2,1,0:T(8,128)(2,1)S(1)} %get-tuple-element.5), channel_id=1, replica_groups=mesh['dp'=64,'ens'=8] {'ens'}, dimensions={0} | all-to-all | bytes 1048576 | tf_op jit(solution)/shard_map/all_to_all | solution.py:32
  89.2 0.1 pad_maximum_fusion
  89.3 104.5 %all-gather.2.cloned.1.call-done = bf16[1024,4096]{1,0:T(8,128)(2,1)} async-done(((bf16[16,4096]{1,0:T(8,128)(2,1)}), bf16[1024,4096]{1,0:T(8,128)(2,1)}) %all-gather.2.cloned.1.call-update) | async-done | bytes 8388624 | tf_op jit(solution)/shard_map/all_gather | solution.py:62
  193.7 0.0 copy-done
  193.8 11.8 %fusion.14 = (bf16[768,128]{1,0:T(8,128)(2,1)S(1)}, f32[768,128]{1,0:T(8,128)S(1)}) fusion(bf16[4096,128]{1,0:T(8,128)(2,1)S(1)} %bitcast.25, bf16[768,1024]{1,0:T(8,128)(2,1)S(1)} %copy-done, bf16[1024,4096]{1,0:T(8,128)(2,1)} %all-gather.2.cloned.1.call-done), kind=kOutput, calls=%fused_computation.25 | convolution fusion | flops 7254147072 | bytes 11599872 | tf_op jit(solution)/shard_map/dot_general | solution.py:66
  205.5 0.0 copy-start.3
  205.6 1.4 broadcast_in_dim.6
  206.9 0.0 copy-start.2
  206.9 11.8 %all-to-all-start.3 = ((bf16[8,768,128]{2,1,0:T(8,128)(2,1)}), bf16[8,768,128]{2,1,0:T(8,128)(2,1)S(1)}, u32[]{:S(2)}, u32[]{:S(2)}) async-start(bf16[8,768,128]{2,1,0:T(8,128)(2,1)} %broadcast_in_dim.6), calls=%async_computation.3 | async-start | bytes 3145728 | tf_op jit(solution)/shard_map/all_to_all | solution.py:38
  218.7 0.0 copy-done.3
  218.7 0.6 fusion.10
  219.3 0.6 dynamic_slice.4
  220.5 0.5 convolution_reduce_fusion.1
  221.0 34.4 %all-to-all-done.3 = bf16[8,768,128]{2,1,0:T(8,128)(2,1)S(1)} async-done(((bf16[8,768,128]{2,1,0:T(8,128)(2,1)}), bf16[8,768,128]{2,1,0:T(8,128)(2,1)S(1)}, u32[]{:S(2)}, u32[]{:S(2)}) %all-to-all-start.3) | async-done | bytes 1572896 | tf_op jit(solution)/shard_map/all_to_all | solution.py:38
  255.4 0.2 convert_reduce_fusion
  255.7 0.0 copy-start.1
  255.7 0.5 convolution_reduce_fusion
  256.1 0.0 copy-done.2
  256.1 1.3 fusion.11
  257.5 1.4 pad_maximum_fusion.1
  258.9 63.6 %all_to_all.39 = f32[64,1,2]{2,1,0:T(1,128)S(1)} all-to-all(f32[64,1,2]{2,1,0:T(1,128)S(1)} %broadcast_in_dim.7), channel_id=1, replica_groups=mesh['dp'=64,'ens'=8] {'dp'}, dimensions={0} | all-to-all | bytes 1024 | tf_op jit(solution)/shard_map/all_to_all | solution.py:38
  322.5 0.1 reduce_sum.49
  322.6 0.6 fusion.13
  324.5 0.0 copy-done.1
  (2 shorter events, 0.1 us)
Async XLA Ops:
  7.2 186.6 %copy-start = (bf16[768,1024]{1,0:T(8,128)(2,1)S(1)}, bf16[768,1024]{1,0:T(8,128)(2,1)}, u32[]{:S(2)}) copy-start(bf16[768,1024]{1,0:T(8,128)(2,1)} %param.5) | copy-start | bytes 4718596
  7.2 186.6 %all-gather.2.cloned.1.call-start = ((), (), s32[]{:S(2)}) async-start(), calls=%async_computation.5 | async-start | bytes 8519680 | tf_op jit(solution)/shard_map/all_gather | solution.py:62
  205.5 13.1 %copy-start.3 = (s32[8]{0:T(128)S(1)}, s32[8]{0:T(128)}, u32[]{:S(2)}) copy-start(s32[8]{0:T(128)} %param.9) | copy-start | bytes 100
  206.9 49.2 %copy-start.2 = (s32[768]{0:T(1024)S(1)}, s32[768]{0:T(1024)}, u32[]{:S(2)}) copy-start(s32[768]{0:T(1024)} %param.6) | copy-start | bytes 9220
  206.9 48.5 %all-to-all-start.3 = ((bf16[8,768,128]{2,1,0:T(8,128)(2,1)}), bf16[8,768,128]{2,1,0:T(8,128)(2,1)S(1)}, u32[]{:S(2)}, u32[]{:S(2)}) async-start(bf16[8,768,128]{2,1,0:T(8,128)(2,1)} %broadcast_in_dim.6), calls=%async_computation.3 | async-start | bytes 3145728 | tf_op jit(solution)/shard_map/all_to_all | solution.py:38
  255.7 68.9 %copy-start.1 = (f32[768,128]{1,0:T(8,128)}, f32[768,128]{1,0:T(8,128)S(1)}, u32[]{:S(2)}) copy-start(f32[768,128]{1,0:T(8,128)S(1)} %broadcast_multiply_fusion) | copy-start | bytes 1179652
Sparse Core Ops, SparseCore 0:
  40.7 153.0 all-gather.1
where the time goes:
time: 334 us
  blocking collectives  144 us (43%)
  waiting for transfers between devices  139 us (42%)
  between operations  18.3 us (5%)
  matrix products  12.7 us (4%)
  starting transfers between devices  11.8 us (4%)
  local copies, waits for them, and re-layouts  4.51 us (1%)
  other arithmetic  3.76 us (1%)
    all_gather x1, waiting for transfers between devices, on_device(): full_first = lax.all_gather(own_first[0], 'dp', axis=0, tiled=True)  104 us
    all_to_all x1, blocking collectives, from_everyone(): return lax.all_to_all(copies, axis, split_axis=0, concat_axis=0, tiled=True)  63.6 us
    all_to_all x2, blocking collectives, several_exchanges(): lax.all_to_all(section, axis, split_axis=0, concat_axis=0, tiled=True)  47.4 us
    all_to_all x1, waiting for transfers between devices, from_everyone(): return lax.all_to_all(copies, axis, split_axis=0, concat_axis=0, tiled=True)  34.4 us
    all_to_all x1, blocking collectives, on_device(): lax.all_to_all(first_weight, 'ens', split_axis=0, concat_axis=2, tiled=True)  32.7 us
    dot_general x1, matrix products, on_device(): jnp.dot(hidden, own_second[0], preferred_element_type=jnp.float32)  11.8 us
    all_to_all x1, starting transfers between devices, from_everyone(): return lax.all_to_all(copies, axis, split_axis=0, concat_axis=0, tiled=True)  11.8 us
  transfers between devices with their start and end apart: 2, of which 2 were waited for; matrix products, arithmetic and copies ran while one was open for 1% of the time, Pallas kernels for 0%

commit v1 on v0

--- a/solution.py
+++ b/solution.py
@@ -59,7 +59,9 @@
     member = lax.axis_index("ens")
     own_first = lax.all_to_all(first_weight, "ens", split_axis=0, concat_axis=2, tiled=True)
     own_second = several_exchanges(second_weight, "ens", 2, 0, 1)
-    full_first = lax.all_gather(own_first[0], "dp", axis=0, tiled=True)
+    full_first = jnp.concatenate(
+        lax.all_to_all(jnp.stack([own_first[0]] * lax.axis_size("dp")), "dp", 0, 0), axis=0
+    )
     hidden = jnp.maximum(
         jnp.dot(embeddings, full_first, preferred_element_type=jnp.float32), 0.0
     ).astype(jnp.bfloat16)

time: 334 us -> 603 us (1.81)
  waiting for transfers between devices: 139 us -> 439 us
  blocking collectives: 144 us -> 68.1 us
  starting transfers between devices: 11.8 us -> 63.3 us
  between operations: 18.3 us -> 4.95 us
    all_to_all x0 -> x3, waiting for transfers between devices: none -> 393 us  [the longest x1 365 us: on_device(): lax.all_to_all(jnp.stack([own_first[0]] * lax.axis_size('dp')), 'dp', 0, 0)]
    all_gather x1 -> x0, waiting for transfers between devices: 104 us -> none  [on_device(): full_first = lax.all_gather(own_first[0], 'dp', axis=0, tiled=True)]
    all_to_all x0 -> x3, starting transfers between devices: none -> 54.6 us  [the longest x1 32.7 us: on_device(): lax.all_to_all(jnp.stack([own_first[0]] * lax.axis_size('dp')), 'dp', 0, 0)]
    all_to_all x1 -> x0, blocking collectives: 32.7 us -> none  [on_device(): lax.all_to_all(first_weight, 'ens', split_axis=0, concat_axis=2, tiled=True)]
    all_to_all x2 -> x1, blocking collectives: 47.4 us -> 19.8 us  [several_exchanges(): lax.all_to_all(section, axis, split_axis=0, concat_axis=0, tiled=True)]
    all_to_all x1, blocking collectives: 63.6 us -> 48.3 us  [from_everyone(): return lax.all_to_all(copies, axis, split_axis=0, concat_axis=0, tiled=True)]
    all_to_all x1, waiting for transfers between devices: 34.4 us -> 46.3 us  [from_everyone(): return lax.all_to_all(copies, axis, split_axis=0, concat_axis=0, tiled=True)]
  transfers between devices with their start and end apart: 2 -> 4, of which waited for: 2 -> 4; matrix products, arithmetic and copies ran while one was open for 1% -> 1% of each run, Pallas kernels for 0% -> 0%
where the time goes in v1:
time: 603 us; the launch traced here: 602 us
  waiting for transfers between devices  439 us (73%)
  blocking collectives  68.1 us (11%)
  starting transfers between devices  63.3 us (10%)
  matrix products  12.9 us (2%)
  local copies, waits for them, and re-layouts  8.92 us (1%)
    all_to_all x1, waiting for transfers between devices, on_device(): lax.all_to_all(jnp.stack([own_first[0]] * lax.axis_size('dp')), 'dp', 0, 0)  365 us
    all_to_all x1, blocking collectives, from_everyone(): return lax.all_to_all(copies, axis, split_axis=0, concat_axis=0, tiled=True)  48.3 us
    all_to_all x1, waiting for transfers between devices, from_everyone(): return lax.all_to_all(copies, axis, split_axis=0, concat_axis=0, tiled=True)  46.3 us
    all_to_all x1, starting transfers between devices, on_device(): lax.all_to_all(jnp.stack([own_first[0]] * lax.axis_size('dp')), 'dp', 0, 0)  32.7 us
    all_to_all x1, blocking collectives, several_exchanges(): lax.all_to_all(section, axis, split_axis=0, concat_axis=0, tiled=True)  19.8 us
    all_to_all x1, starting transfers between devices, on_device(): lax.all_to_all(first_weight, 'ens', split_axis=0, concat_axis=2, tiled=True)  18.4 us
    all_to_all x1, waiting for transfers between devices, several_exchanges(): lax.all_to_all(section, axis, split_axis=0, concat_axis=0, tiled=True)  16.2 us
    all_to_all x1, waiting for transfers between devices, on_device(): lax.all_to_all(first_weight, 'ens', split_axis=0, concat_axis=2, tiled=True)  12.2 us
  transfers between devices with their start and end apart: 4, of which 4 were waited for; matrix products, arithmetic and copies ran while one was open for 1% of the time, Pallas kernels for 0%

profile of v1, /device:TPU:1, one launch (start us, length us, event | category | flops | bytes accessed | tf_op | source)
XLA Modules:
  0.0 602.1 jit_solution(1657625365680144362)
XLA Ops:
  0.6 0.0 copy-start
  0.6 18.4 %all-to-all-start = ((bf16[8,16,512]{2,1,0:T(8,128)(2,1)}), bf16[8,16,512]{2,1,0:T(8,128)(2,1)S(1)}, u32[]{:S(2)}, u32[]{:S(2)}) async-start(bf16[8,16,512]{2,1,0:T(8,128)(2,1)} %param.7), calls=%async_computation | async-start | bytes 262144 | tf_op jit(solution)/shard_map/all_to_all | solution.py:60
  19.0 2.1 fusion.12
  21.1 12.2 %all-to-all-done = bf16[8,16,512]{2,1,0:T(8,128)(2,1)S(1)} async-done(((bf16[8,16,512]{2,1,0:T(8,128)(2,1)}), bf16[8,16,512]{2,1,0:T(8,128)(2,1)S(1)}, u32[]{:S(2)}, u32[]{:S(2)}) %all-to-all-start) | async-done | bytes 131104 | tf_op jit(solution)/shard_map/all_to_all | solution.py:60
  33.3 19.8 %all_to_all.44 = bf16[8,1,256,128]{3,2,1,0:T(8,128)(2,1)S(1)} all-to-all(bf16[8,1,256,128]{3,2,1,0:T(8,128)(2,1)S(1)} %get-tuple-element.6), channel_id=1, replica_groups=mesh['dp'=64,'ens'=8] {'ens'}, dimensions={0} | all-to-all | bytes 1048576 | tf_op jit(solution)/shard_map/all_to_all | solution.py:32
  53.1 3.5 all-to-all-start.2
  56.6 16.2 %all-to-all-done.2 = bf16[8,1,256,128]{3,2,1,0:T(8,128)(2,1)S(1)} async-done(((bf16[8,1,256,128]{3,2,1,0:T(8,128)(2,1)}), bf16[8,1,256,128]{3,2,1,0:T(8,128)(2,1)S(1)}, u32[]{:S(2)}, u32[]{:S(2)}) %all-to-all-start.2) | async-done | bytes 524320 | tf_op jit(solution)/shard_map/all_to_all | solution.py:32
  72.8 4.3 stack.3
  77.1 32.7 %all-to-all-start.1 = ((bf16[64,16,4096]{2,1,0:T(8,128)(2,1)}), bf16[64,16,4096]{2,1,0:T(8,128)(2,1)}, u32[]{:S(2)}, u32[]{:S(2)}) async-start(bf16[64,16,4096]{2,1,0:T(8,128)(2,1)} %stack.3), calls=%async_computation.1 | async-start | bytes 16777216 | tf_op jit(solution)/shard_map/all_to_all | solution.py:63
  109.7 1.1 pad_maximum_fusion
  110.8 364.6 %all-to-all-done.1 = bf16[64,16,4096]{2,1,0:T(8,128)(2,1)} async-done(((bf16[64,16,4096]{2,1,0:T(8,128)(2,1)}), bf16[64,16,4096]{2,1,0:T(8,128)(2,1)}, u32[]{:S(2)}, u32[]{:S(2)}) %all-to-all-start.1) | async-done | bytes 8388640 | tf_op jit(solution)/shard_map/all_to_all | solution.py:63
  475.4 0.0 copy-done
  475.4 12.0 %fusion.14 = (bf16[768,128]{1,0:T(8,128)(2,1)S(1)}, f32[768,128]{1,0:T(8,128)S(1)}) fusion(bf16[4096,128]{1,0:T(8,128)(2,1)} %bitcast.26, bf16[768,1024]{1,0:T(8,128)(2,1)S(1)} %copy-done, bf16[1024,4096]{1,0:T(8,128)(2,1)} %bitcast.2), kind=kOutput, calls=%fused_computation.25 | convolution fusion | flops 7254147072 | bytes 11599872 | tf_op jit(solution)/shard_map/dot_general | solution.py:68
  487.4 0.0 copy-start.3
  487.4 1.4 broadcast_in_dim.6
  488.8 0.0 copy-start.2
  488.8 8.7 %all-to-all-start.4 = ((bf16[8,768,128]{2,1,0:T(8,128)(2,1)}), bf16[8,768,128]{2,1,0:T(8,128)(2,1)S(1)}, u32[]{:S(2)}, u32[]{:S(2)}) async-start(bf16[8,768,128]{2,1,0:T(8,128)(2,1)} %broadcast_in_dim.6), calls=%async_computation.4 | async-start | bytes 3145728 | tf_op jit(solution)/shard_map/all_to_all | solution.py:38
  497.5 0.0 copy-done.3
  497.5 0.6 fusion.10
  498.1 0.6 dynamic_slice.4
  499.4 0.5 convolution_reduce_fusion.1
  499.8 46.3 %all-to-all-done.4 = bf16[8,768,128]{2,1,0:T(8,128)(2,1)S(1)} async-done(((bf16[8,768,128]{2,1,0:T(8,128)(2,1)}), bf16[8,768,128]{2,1,0:T(8,128)(2,1)S(1)}, u32[]{:S(2)}, u32[]{:S(2)}) %all-to-all-start.4) | async-done | bytes 1572896 | tf_op jit(solution)/shard_map/all_to_all | solution.py:38
  546.1 0.2 convert_reduce_fusion
  546.4 0.0 copy-start.1
  546.4 0.5 convolution_reduce_fusion
  546.8 0.0 copy-done.2
  546.9 1.3 fusion.11
  548.2 1.4 pad_maximum_fusion.1
  549.6 48.3 %all_to_all.45 = f32[64,1,2]{2,1,0:T(1,128)S(1)} all-to-all(f32[64,1,2]{2,1,0:T(1,128)S(1)} %broadcast_in_dim.7), channel_id=1, replica_groups=mesh['dp'=64,'ens'=8] {'dp'}, dimensions={0} | all-to-all | bytes 1024 | tf_op jit(solution)/shard_map/all_to_all | solution.py:38
  597.9 0.1 reduce_sum.49
  598.0 0.6 fusion.13
  599.9 0.0 copy-done.1
  (3 shorter events, 0.1 us)
Async XLA Ops:
  0.6 474.8 %copy-start = (bf16[768,1024]{1,0:T(8,128)(2,1)S(1)}, bf16[768,1024]{1,0:T(8,128)(2,1)}, u32[]{:S(2)}) copy-start(bf16[768,1024]{1,0:T(8,128)(2,1)} %param.5) | copy-start | bytes 4718596
  0.6 32.7 %all-to-all-start = ((bf16[8,16,512]{2,1,0:T(8,128)(2,1)}), bf16[8,16,512]{2,1,0:T(8,128)(2,1)S(1)}, u32[]{:S(2)}, u32[]{:S(2)}) async-start(bf16[8,16,512]{2,1,0:T(8,128)(2,1)} %param.7), calls=%async_computation | async-start | bytes 262144 | tf_op jit(solution)/shard_map/all_to_all | solution.py:60
  53.1 19.7 %all-to-all-start.2 = ((bf16[8,1,256,128]{3,2,1,0:T(8,128)(2,1)}), bf16[8,1,256,128]{3,2,1,0:T(8,128)(2,1)S(1)}, u32[]{:S(2)}, u32[]{:S(2)}) async-start(bf16[8,1,256,128]{3,2,1,0:T(8,128)(2,1)} %get-tuple-element.5), calls=%async_computation.2 | async-start | bytes 1048576 | tf_op jit(solution)/shard_map/all_to_all | solution.py:32
  77.1 398.3 %all-to-all-start.1 = ((bf16[64,16,4096]{2,1,0:T(8,128)(2,1)}), bf16[64,16,4096]{2,1,0:T(8,128)(2,1)}, u32[]{:S(2)}, u32[]{:S(2)}) async-start(bf16[64,16,4096]{2,1,0:T(8,128)(2,1)} %stack.3), calls=%async_computation.1 | async-start | bytes 16777216 | tf_op jit(solution)/shard_map/all_to_all | solution.py:63
  487.4 10.1 %copy-start.3 = (s32[8]{0:T(128)S(1)}, s32[8]{0:T(128)}, u32[]{:S(2)}) copy-start(s32[8]{0:T(128)} %param.9) | copy-start | bytes 100
  488.8 58.1 %copy-start.2 = (s32[768]{0:T(1024)S(1)}, s32[768]{0:T(1024)}, u32[]{:S(2)}) copy-start(s32[768]{0:T(1024)} %param.6) | copy-start | bytes 9220
  488.8 57.3 %all-to-all-start.4 = ((bf16[8,768,128]{2,1,0:T(8,128)(2,1)}), bf16[8,768,128]{2,1,0:T(8,128)(2,1)S(1)}, u32[]{:S(2)}, u32[]{:S(2)}) async-start(bf16[8,768,128]{2,1,0:T(8,128)(2,1)} %broadcast_in_dim.6), calls=%async_computation.4 | async-start | bytes 3145728 | tf_op jit(solution)/shard_map/all_to_all | solution.py:38
  546.4 53.5 %copy-start.1 = (f32[768,128]{1,0:T(8,128)}, f32[768,128]{1,0:T(8,128)S(1)}, u32[]{:S(2)}) copy-start(f32[768,128]{1,0:T(8,128)S(1)} %broadcast_multiply_fusion) | copy-start | bytes 1179652
